TPU v7x, 512 devices: a whole 4x4x16 slice. The times are simulated.
512 devices in a mesh: grp: 64 (over z, x_lo, core), tp: 8 (over x_hi, y).
Axes of the slice: x: 4 (x_hi: 2, x_lo: 2; x = x_hi * 2 + x_lo), y: 4, z: 16, core: 2. Of those that a mesh axis runs over, the one named last changes fastest.
Arguments:
- memory_rows: bfloat16 [65536, 4096], P('grp', 'tp'), may hold values from -24 to 24, as said below
- norm_gain: float32 [4096], replicated, may hold values from 0.25 to 1.75
- key_weight: bfloat16 [4096, 4096], P(None, 'tp'), may hold values from -0.09375 to 0.09375
- owner_table: int32 [8192], replicated, may hold values from 0 to 8191, as said below
Outputs:
- placed_keys: bfloat16 [65536, 4096], P('grp', 'tp')
Inputs may be any that keep to these rules, and one draw needn't show every extreme that they name: A permutation of the 8192 block numbers. Block b of the input goes to block position owner_table[b], which lies in group owner_table[b] // 128. The 128 blocks of one group go to all 64 groups, exactly 2 blocks to each of them. `memory_rows`: rows have offsets and scales of their own, and features a common pattern.
All inputs are finite; a program needn't handle non-finite values.
Results may differ from a plain program's by a relative error of at most 0.0049.
Values may be sent and summed in bfloat16 or wider, within the bound.
A program may use at most 64 MiB of HBM per device.

v0:
```python
import jax
import jax.numpy as jnp
from jax import lax
from jax.sharding import PartitionSpec as P

BLK_ROWS = 8


EPS = 1e-05


def to_owners(block_rows, owner_table):
    groups = lax.axis_size("grp")
    position = lax.axis_index("grp")
    row_count, col_count = block_rows.shape
    blocks_here = row_count // BLK_ROWS
    capacity = max(1, blocks_here // groups)
    owned_slots = lax.dynamic_slice_in_dim(owner_table, position * blocks_here, blocks_here)
    target = owned_slots // blocks_here
    block_ids = jnp.arange(blocks_here, dtype=jnp.int32)
    earlier = (target[None, :] == target[:, None]) & (block_ids[None, :] < block_ids[:, None])
    rank = jnp.sum(earlier.astype(jnp.int32), axis=1)
    send_slot = target * capacity + rank
    slot_ids = jnp.arange(groups * capacity, dtype=jnp.int32)
    sender = (send_slot[None, :] == slot_ids[:, None]).astype(jnp.bfloat16)
    flattened = block_rows.reshape(blocks_here, BLK_ROWS * col_count)
    outgoing = jnp.dot(sender, flattened, preferred_element_type=jnp.float32).astype(jnp.bfloat16)
    incoming = lax.all_to_all(outgoing, "grp", split_axis=0, concat_axis=0, tiled=True)
    block_total = owner_table.shape[0]
    inverse = (
        jnp.zeros((block_total,), jnp.int32)
        .at[owner_table]
        .set(jnp.arange(block_total, dtype=jnp.int32))
    )
    arriving = lax.dynamic_slice_in_dim(inverse, position * blocks_here, blocks_here)
    anchor_group = arriving // blocks_here
    anchor_column = arriving % blocks_here
    target_table = owner_table.reshape(groups, blocks_here) // blocks_here
    anchor_targets = target_table[anchor_group]
    before = (anchor_targets == position) & (block_ids[None, :] < anchor_column[:, None])
    anchor_rank = jnp.sum(before.astype(jnp.int32), axis=1)
    source_slot = anchor_group * capacity + anchor_rank
    picker = (source_slot[:, None] == slot_ids[None, :]).astype(jnp.bfloat16)
    placed = jnp.dot(picker, incoming, preferred_element_type=jnp.float32).astype(jnp.bfloat16)
    return placed.reshape(row_count, col_count)


def project(memory_rows, norm_gain, key_weight):
    width = norm_gain.shape[0]
    whole_rows = lax.all_gather(memory_rows, "tp", axis=1, tiled=True)
    values = whole_rows.astype(jnp.float32)
    row_mean = jnp.sum(values, axis=1, keepdims=True) / width
    row_var = jnp.sum(values * values, axis=1, keepdims=True) / width - row_mean * row_mean
    normed = ((values - row_mean) * lax.rsqrt(row_var + EPS) * norm_gain[None, :]).astype(
        jnp.bfloat16
    )
    keys = jnp.dot(normed, key_weight, preferred_element_type=jnp.float32)
    return keys.astype(jnp.bfloat16)


def on_device(memory_rows, norm_gain, key_weight, owner_table):
    keys = project(memory_rows, norm_gain, key_weight)
    return to_owners(keys, owner_table)


def solution(mesh):
    in_specs = (P("grp", "tp"), P(), P(None, "tp"), P())
    out_specs = P("grp", "tp")
    return jax.shard_map(
        on_device, mesh=mesh, in_specs=in_specs, out_specs=out_specs, check_vma=False
    )
```

profile of v0, /device:TPU:1, one launch (start us, length us, event | category | flops | bytes accessed | tf_op | source)
XLA Modules:
  0.0 235.4 jit_solution(608830909230115830)
XLA Ops:
  6.5 0.0 copy-start.2
  6.5 0.0 all-gather.2.cloned.1.call-start
  6.5 0.7 all-gather.2.cloned.1.call-update
  7.3 0.8 and_select_fusion
  8.0 0.2 convert_reduce_fusion.1
  8.2 0.8 multiply_add_fusion
  9.0 133.8 %all-gather.2.cloned.1.call-done = bf16[1024,4096]{1,0:T(8,128)(2,1)} async-done(((bf16[1024,512]{1,0:T(8,128)(2,1)}), bf16[1024,4096]{1,0:T(8,128)(2,1)}) %all-gather.2.cloned.1.call-update) | async-done | bytes 8388624 | tf_op jit(solution)/shard_map/all_gather | solution.py:50
  142.8 0.0 copy-start
  142.8 6.1 %convert_reduce_fusion = (f32[1024]{0:T(1024)S(1)}, f32[1024]{0:T(1024)S(1)}) fusion(bf16[1024,4096]{1,0:T(8,128)(2,1)} %all-gather.2.cloned.1.call-done), kind=kLoop, calls=%fused_computation.4 | loop fusion | flops 16775168 | bytes 8396800 | tf_op jit(solution)/shard_map/reduce_sum | solution.py:52
  148.9 0.0 copy-done.2
  148.9 0.0 copy-done
  149.0 6.8 %fusion.9 = bf16[1024,512]{1,0:T(8,128)(2,1)S(1)} fusion(bf16[4096,512]{1,0:T(8,128)(2,1)} %param.6, bf16[1024,4096]{1,0:T(8,128)(2,1)S(1)} %copy-done, f32[4096]{0:T(1024)S(1)} %copy-done.2, f32[1024]{0:T(1024)S(1)} %get-tuple-element.12, f32[1024]{0:T(1024)S(1)} %get-tuple-element.11), kind=kOutput, calls=%fused_computation.15 | convolution fusion | flops 4316463104 | bytes 13656064 | tf_op jit(solution)/shard_map/dot_general | solution.py:57
  155.8 0.0 copy-start.1
  155.8 0.5 reshape.36
  156.3 0.4 convolution_convert_fusion.1
  156.8 1.5 all_to_all.8
  158.3 14.1 %all-to-all-start = ((bf16[64,2,4096]{2,1,0:T(2,128)(2,1)}), bf16[64,2,4096]{2,1,0:T(2,128)(2,1)S(1)}, u32[]{:S(2)}, u32[]{:S(2)}) async-start(bf16[64,2,4096]{2,1,0:T(2,128)(2,1)} %all_to_all.8), calls=%async_computation | async-start | bytes 2097152 | tf_op jit(solution)/shard_map/all_to_all | solution.py:28
  172.4 0.0 copy-done.1
  172.5 30.5 %scatter_custom_fusion = s32[8192]{0:T(1024)S(1)} fusion(s32[8192]{0:T(1024)S(1)} %compare_select_fusion, s32[8192]{0:T(1024)S(1)} %iota.11, s32[]{:T(128)} %constant.54.clone.1), kind=kCustom, calls=%fused_computation.36 | custom fusion | bytes 32772 | tf_op jit(solution)/shard_map/scatter | solution.py:33
  202.9 0.1 and_select_fusion.1
  203.0 0.1 compare_select_fusion.1
  203.2 0.6 gather_fusion
  203.8 0.2 convert_reduce_fusion.2
  204.0 22.3 %all-to-all-done = bf16[64,2,4096]{2,1,0:T(2,128)(2,1)S(1)} async-done(((bf16[64,2,4096]{2,1,0:T(2,128)(2,1)}), bf16[64,2,4096]{2,1,0:T(2,128)(2,1)S(1)}, u32[]{:S(2)}, u32[]{:S(2)}) %all-to-all-start) | async-done | bytes 1048608 | tf_op jit(solution)/shard_map/all_to_all | solution.py:28
  226.3 0.4 all_to_all.10
  226.7 0.5 convolution_convert_fusion
  227.2 1.3 reshape.37
  (6 shorter events, 0.1 us)
Async XLA Ops:
  6.5 142.4 %copy-start.2 = (f32[4096]{0:T(1024)S(1)}, f32[4096]{0:T(1024)}, u32[]{:S(2)}) copy-start(f32[4096]{0:T(1024)} %param.5) | copy-start | bytes 49156
  6.5 136.3 %all-gather.2.cloned.1.call-start = ((), (), s32[]{:S(2)}) async-start(), calls=%async_computation.1 | async-start | bytes 9437184 | tf_op jit(solution)/shard_map/all_gather | solution.py:50
  142.8 6.1 %copy-start = (bf16[1024,4096]{1,0:T(8,128)(2,1)S(1)}, bf16[1024,4096]{1,0:T(8,128)(2,1)}, u32[]{:S(2)}) copy-start(bf16[1024,4096]{1,0:T(8,128)(2,1)} %all-gather.2.cloned.1.call-done) | copy-start | bytes 25165828
  155.8 16.6 %copy-start.1 = (s32[8192]{0:T(1024)S(1)}, s32[8192]{0:T(1024)}, u32[]{:S(2)}) copy-start(s32[8192]{0:T(1024)} %param.7) | copy-start | bytes 98308
  158.3 68.0 %all-to-all-start = ((bf16[64,2,4096]{2,1,0:T(2,128)(2,1)}), bf16[64,2,4096]{2,1,0:T(2,128)(2,1)S(1)}, u32[]{:S(2)}, u32[]{:S(2)}) async-start(bf16[64,2,4096]{2,1,0:T(2,128)(2,1)} %all_to_all.8), calls=%async_computation | async-start | bytes 2097152 | tf_op jit(solution)/shard_map/all_to_all | solution.py:28
Sparse Core Ops, SparseCore 0:
  10.4 132.3 all-gather.1
where the time goes:
time: 237 us; the launch traced here: 235 us
  waiting for transfers between devices  157 us (66%)
  local copies, waits for them, and re-layouts  34.9 us (15%)
  starting transfers between devices  14.1 us (6%)
  between operations  13.5 us (6%)
  other arithmetic  8.2 us (3%)
  matrix products  7.74 us (3%)
    all_gather x1, waiting for transfers between devices, project(): whole_rows = lax.all_gather(memory_rows, 'tp', axis=1, tiled=True)  134 us
    scatter x1, local copies, waits for them, and re-layouts, to_owners(): inverse = jnp.zeros((block_total,), jnp.int32).at[owner_table].set(jnp.ar...  30.5 us
    all_to_all x1, waiting for transfers between devices, to_owners(): lax.all_to_all(outgoing, 'grp', split_axis=0, concat_axis=0, tiled=True)  22.3 us
    all_to_all x1, starting transfers between devices, to_owners(): lax.all_to_all(outgoing, 'grp', split_axis=0, concat_axis=0, tiled=True)  14.1 us
    dot_general x1, matrix products, project(): keys = jnp.dot(normed, key_weight, preferred_element_type=jnp.float32)  6.84 us
    reduce_sum x1, other arithmetic, project(): row_mean = jnp.sum(values, axis=1, keepdims=True) / width  6.09 us
  transfers between devices with their start and end apart: 2, of which 2 were waited for; matrix products, arithmetic and copies ran while one was open for 14% of the time, Pallas kernels for 0%

commit v1 on v0

v1 whole, which is shorter than its diff:
```python
import functools

import jax
import jax.numpy as jnp
from jax import lax
from jax.experimental import pallas as pl
from jax.experimental.pallas import tpu as pltpu
from jax.sharding import PartitionSpec as P

BLK_ROWS = 8
EPS = 1e-05
MESH = pl.DeviceIdType.MESH

CPC = 2
FIRST = 5
BURST = 3


def class_shift(q, depth):
    return lax.rem(((q + 1) // 2) * (2 * lax.rem(q, 2) - 1) + depth, depth)


def tables(owner_table, depth):
    g = lax.axis_index("grp")
    z, xl, co = g // 4, (g // 2) % 2, g % 2
    blocks = 8 * depth
    groups = 4 * depth
    table = owner_table.reshape(groups, blocks)
    target = table // blocks
    own = lax.dynamic_slice_in_dim(target, g, 1, axis=0)[0]
    ids = jnp.arange(blocks, dtype=jnp.int32)
    rank = jnp.sum(
        ((own[None, :] == own[:, None]) & (ids[None, :] < ids[:, None])).astype(jnp.int32), axis=1
    )
    r = ids % 2
    k = (ids // 2) % CPC
    m = (ids // (2 * CPC)) % 4
    c = ids // (8 * CPC)
    q = c * CPC + k
    dz = ((q + 1) // 2) * (2 * (q % 2) - 1)
    dest = ((z + dz + depth) % depth) * 4 + m
    hit = (own[None, :] == dest[:, None]) & (rank[None, :] == r[:, None])
    order = jnp.sum(jnp.where(hit, ids[None, :], 0), axis=1)

    mine = target == g
    slot = table % blocks
    column = jnp.where(mine, ids[None, :], blocks)
    first = jnp.min(column, axis=1, keepdims=True)
    slot_first = jnp.sum(jnp.where(ids[None, :] == first, slot, 0), axis=1)
    slot_both = jnp.sum(jnp.where(mine, slot, 0), axis=1)
    slots = jnp.concatenate([slot_first, slot_both - slot_first])
    src = jnp.arange(2 * groups, dtype=jnp.int32) % groups
    which = jnp.arange(2 * groups, dtype=jnp.int32) // groups
    back = (z - src // 4 + depth) % depth
    q = jnp.where(back <= depth // 2, jnp.maximum(2 * back - 1, 0), 2 * (depth - back))
    dl = ((src // 2) % 2 + xl) % 2
    dc = (src % 2 + co) % 2
    where = (((q // CPC) * 4 + dl * 2 + dc) * CPC + q % CPC) * 2 + which
    place = jnp.sum(jnp.where(slots[None, :] == ids[:, None], where[None, :], 0), axis=1)
    return order, place


def flip(bit, by):
    return 1 - bit if by else bit


def refresh_kernel(
    depth,
    order,
    x_hbm,
    gain,
    w_hbm,
    found,
    xin,
    sorted_rows,
    gat,
    w_own,
    w_far,
    stats,
    part,
    arrived,
    load_sem,
    w_load_sem,
    z_send,
    z_recv,
    y_send,
    y_recv,
    r_send,
    r_recv,
    s_send,
    s_recv,
    x_send,
    x_recv,
    w_send,
    w_recv,
    d_send,
    d_recv,
):
    g, t = lax.axis_index("grp"), lax.axis_index("tp")
    z, xl, co = g // 4, lax.rem(g // 2, 2), lax.rem(g, 2)
    xh, y = t // 4, lax.rem(t, 4)
    chunks = depth // CPC
    dl_width = x_hbm.shape[-1]
    features = 8 * dl_width
    half_rows = 4 * dl_width
    rows_c = 64 * CPC

    def device(zz, xxl, cc, xxh, yy):
        return {"grp": zz * 4 + xxl * 2 + cc, "tp": xxh * 4 + yy}

    load = pltpu.make_async_copy(x_hbm, xin, load_sem)
    load.start()
    w_start = pl.multiple_of(xh * half_rows, half_rows)
    load_w = pltpu.make_async_copy(w_hbm.at[pl.ds(w_start, half_rows)], w_own, w_load_sem)
    load_w.start()

    barrier = pltpu.get_barrier_semaphore()
    partners = 0
    for step in range(1, depth):
        pl.semaphore_signal(
            barrier, inc=1, device_id=device(lax.rem(z + step, depth), xl, co, xh, y), device_id_type=MESH
        )
        partners += 1
    for step in range(1, 8):
        pl.semaphore_signal(
            barrier, inc=1, device_id={"grp": g, "tp": lax.rem(t + step, 8)}, device_id_type=MESH
        )
        partners += 1
    for j in range(1, 8):
        if j == 4:
            continue
        pl.semaphore_signal(
            barrier,
            inc=1,
            device_id=device(z, flip(xl, (j // 2) % 2), flip(co, j % 2), flip(xh, j // 4), y),
            device_id_type=MESH,
        )
        partners += 1

    load.wait()

    def sort_step(s, carry):
        cc = s // (8 * CPC)
        mm = lax.rem(s // (2 * CPC), 4)
        kk = lax.rem(s // 2, CPC)
        sorted_rows[cc, mm, kk, lax.rem(s, 2)] = xin[order[s]]
        return carry

    lax.fori_loop(0, 8 * depth, sort_step, 0, unroll=8)
    gat[y, 0, :, 0] = sorted_rows[0, :, 0]

    pl.semaphore_wait(barrier, partners)

    def z_copy(q):
        cc, kk = q // CPC, lax.rem(q, CPC)
        return pltpu.make_async_remote_copy(
            src_ref=sorted_rows.at[cc, :, kk],
            dst_ref=gat.at[y, cc, :, kk],
            send_sem=z_send.at[q],
            recv_sem=z_recv.at[q],
            device_id=device(lax.rem(z + class_shift(q, depth), depth), xl, co, xh, y),
            device_id_type=MESH,
        )

    def z_start(q, carry):
        z_copy(q).start()
        return carry

    lax.fori_loop(1, depth, z_start, 0)

    w_rows = half_rows // 2
    w_at = pl.multiple_of(co * w_rows, w_rows)
    w_copy = pltpu.make_async_remote_copy(
        src_ref=w_hbm.at[pl.ds(pl.multiple_of((1 - xh) * half_rows + w_at, w_rows), w_rows)],
        dst_ref=w_far.at[pl.ds(w_at, w_rows)],
        send_sem=w_send,
        recv_sem=w_recv,
        device_id=device(z, 1 - xl, co, 1 - xh, y),
        device_id_type=MESH,
    )
    w_copy.start()
    w_share = pltpu.make_async_remote_copy(
        src_ref=w_far.at[pl.ds(w_at, w_rows)],
        dst_ref=w_far.at[pl.ds(w_at, w_rows)],
        send_sem=d_send,
        recv_sem=d_recv,
        device_id=device(z, xl, 1 - co, xh, y),
        device_id_type=MESH,
    )

    left, right = lax.rem(y + 3, 4), lax.rem(y + 1, 4)

    def y_copy(side, c):
        return pltpu.make_async_remote_copy(
            src_ref=gat.at[y, c],
            dst_ref=gat.at[y, c],
            send_sem=y_send.at[side, c],
            recv_sem=y_recv.at[side, c],
            device_id=device(z, xl, co, xh, right if side == 0 else left),
            device_id_type=MESH,
        )

    def relay_copy(side, c):
        span = pl.ds(0, 2) if side == 0 else pl.ds(2, 2)
        piece = left if side == 0 else right
        return pltpu.make_async_remote_copy(
            src_ref=gat.at[piece, c, span],
            dst_ref=gat.at[piece, c, span],
            send_sem=r_send.at[side, c],
            recv_sem=r_recv.at[side, c],
            device_id=device(z, xl, co, xh, right if side == 0 else left),
            device_id_type=MESH,
        )

    def stats_copy(c, step):
        return pltpu.make_async_remote_copy(
            src_ref=stats.at[c, 0],
            dst_ref=stats.at[c, step],
            send_sem=s_send.at[c],
            recv_sem=s_recv.at[c],
            device_id={"grp": g, "tp": lax.rem(t + step, 8)},
            device_id_type=MESH,
        )

    def x_copy(c, j):
        dh, dl, dc = j // 4, (j // 2) % 2, j % 2
        to_l, to_c = flip(xl, dl), flip(co, dc)
        return pltpu.make_async_remote_copy(
            src_ref=part.at[c, dh, to_l * 2 + to_c],
            dst_ref=arrived.at[c, j],
            send_sem=x_send.at[c],
            recv_sem=x_recv.at[c],
            device_id=device(z, to_l, to_c, flip(xh, dh), y),
            device_id_type=MESH,
        )

    def take(c):
        for kk in range(CPC):
            q = c * CPC + kk
            if kk == 0:

                @pl.when(c > 0)
                def _():
                    z_copy(q).wait_recv()

            else:
                z_copy(q).wait_recv()
        y_copy(0, c).start()
        y_copy(1, c).start()
        v = gat[y, c].astype(jnp.float32).reshape(rows_c, dl_width)
        row_sum = jnp.sum(v, axis=1, keepdims=True)
        row_sq = jnp.sum(v * v, axis=1, keepdims=True)
        lane = lax.broadcasted_iota(jnp.int32, (rows_c, 128), 1)
        both = jnp.where(lane == 0, row_sum, jnp.where(lane == 1, row_sq, 0.0))
        stats[c, 0, :, pl.ds(0, rows_c)] = both.T[0:8, :]
        for step in range(1, 8):
            stats_copy(c, step).start()

    def relay(c):
        y_copy(0, c).wait_recv()
        relay_copy(0, c).start()
        y_copy(1, c).wait_recv()
        relay_copy(1, c).start()

    def multiply(c):
        relay_copy(0, c).wait_recv()
        relay_copy(1, c).wait_recv()
        all_stats = stats.at[c, pl.ds(1, 7)]
        pltpu.make_async_copy(all_stats, all_stats, s_recv.at[c]).wait()
        total = jnp.sum(stats[c], axis=0)[:, 0:rows_c]
        mean = total[0:1] / features
        var = total[1:2] / features - mean * mean
        rstd = lax.rsqrt(var + EPS)
        sub = lax.broadcasted_iota(jnp.int32, (128, rows_c), 0)
        columns = jnp.where(sub == 0, mean, rstd).T
        mean_c, rstd_c = columns[:, 0:1], columns[:, 1:2]
        near = jnp.zeros((rows_c, dl_width), jnp.float32)
        far = jnp.zeros((rows_c, dl_width), jnp.float32)
        for yy in range(4):
            v = gat[yy, c].astype(jnp.float32).reshape(rows_c, dl_width)
            scale = gain[0:1, pl.ds(pl.multiple_of(w_start + yy * dl_width, dl_width), dl_width)]
            normed = ((v - mean_c) * rstd_c * scale).astype(jnp.bfloat16)
            span = pl.ds(yy * dl_width, dl_width)
            near += jnp.dot(normed, w_own[span, :], preferred_element_type=jnp.float32)
            far += jnp.dot(normed, w_far[span, :], preferred_element_type=jnp.float32)
        shape = (4, CPC * 2, BLK_ROWS, dl_width)
        part[c, 0] = near.reshape(shape).astype(jnp.bfloat16)
        part[c, 1] = far.reshape(shape).astype(jnp.bfloat16)
        for j in range(1, 8):
            x_copy(c, j).start()

    def add(c):
        incoming = arrived.at[c, pl.ds(1, 7)]
        pltpu.make_async_copy(incoming, incoming, x_recv.at[c]).wait()
        for e in range(4):
            if e == 0:
                a = part[c, 0, xl * 2 + co]
            else:
                a = arrived[c, e]
            b = arrived[c, 4 + e]
            found[c, e] = (a.astype(jnp.float32) + b.astype(jnp.float32)).astype(jnp.bfloat16)

    def done(i):
        ahead = jnp.minimum(jnp.maximum((i - (FIRST - 1)) * BURST, 0), jnp.maximum(i - 1, 0))
        return jnp.minimum(ahead, chunks)

    def loop(i, carry):
        @pl.when(i == FIRST)
        def _():
            w_copy.wait_recv()
            w_share.start()
            load_w.wait()
            w_share.wait_recv()

        @pl.when(i >= FIRST)
        def _():
            lax.fori_loop(done(i - 1), done(i), lambda c, a: (multiply(c), a)[1], 0)

        @pl.when(i >= FIRST + 1)
        def _():
            lax.fori_loop(done(i - 2), done(i - 1), lambda c, a: (add(c), a)[1], 0)

        @pl.when(jnp.logical_and(i >= 1, i <= chunks))
        def _():
            relay(i - 1)

        @pl.when(i < chunks)
        def _():
            take(i)

        return carry

    lax.fori_loop(0, chunks + 3, loop, 0)

    def drain(c, carry):
        for side in range(2):
            y_copy(side, c).wait_send()
            relay_copy(side, c).wait_send()
        sent = stats.at[c, pl.ds(1, 7)]
        pltpu.make_async_copy(sent, sent, s_send.at[c]).wait()
        gone = arrived.at[c, pl.ds(1, 7)]
        pltpu.make_async_copy(gone, gone, x_send.at[c]).wait()
        return carry

    lax.fori_loop(0, chunks, drain, 0)

    def z_drain(q, carry):
        z_copy(q).wait_send()
        return carry

    lax.fori_loop(1, depth, z_drain, 0)
    w_copy.wait_send()
    w_share.wait_send()


def refresh(depth, order, rows, gain, weight):
    chunks = depth // CPC
    blocks, _, width = rows.shape
    bf16 = jnp.bfloat16
    dma = pltpu.SemaphoreType.DMA
    any_space = pl.BlockSpec(memory_space=pl.ANY)
    return pl.pallas_call(
        functools.partial(refresh_kernel, depth),
        out_shape=jax.ShapeDtypeStruct((chunks, 4, CPC * 2, BLK_ROWS, width), bf16),
        in_specs=[
            pl.BlockSpec(memory_space=pltpu.SMEM),
            any_space,
            pl.BlockSpec(memory_space=pltpu.VMEM),
            any_space,
        ],
        out_specs=pl.BlockSpec(memory_space=pltpu.VMEM),
        scratch_shapes=[
            pltpu.VMEM((blocks, BLK_ROWS, width), bf16),
            pltpu.VMEM((chunks, 4, CPC, 2, BLK_ROWS, width), bf16),
            pltpu.VMEM((4, chunks, 4, CPC, 2, BLK_ROWS, width), bf16),
            pltpu.VMEM((4 * width, width), bf16),
            pltpu.VMEM((4 * width, width), bf16),
            pltpu.VMEM((chunks, 8, 8, 128), jnp.float32),
            pltpu.VMEM((chunks, 2, 4, CPC * 2, BLK_ROWS, width), bf16),
            pltpu.VMEM((chunks, 8, CPC * 2, BLK_ROWS, width), bf16),
            dma,
            dma,
            dma((depth,)),
            dma((depth,)),
            dma((2, chunks)),
            dma((2, chunks)),
            dma((2, chunks)),
            dma((2, chunks)),
            dma((chunks,)),
            dma((chunks,)),
            dma((chunks,)),
            dma((chunks,)),
            dma,
            dma,
            dma,
            dma,
        ],
        compiler_params=pltpu.CompilerParams(
            collective_id=0, has_side_effects=True, vmem_limit_bytes=60 * 1024 * 1024
        ),
        name="refresh",
    )(order, rows, gain, weight)


def place_kernel(place, found, out):
    def step(p, carry):
        out[p] = found[place[p]]
        return carry

    lax.fori_loop(0, out.shape[0], step, 0, unroll=8)


def place_blocks(place, found):
    return pl.pallas_call(
        place_kernel,
        out_shape=jax.ShapeDtypeStruct(found.shape, found.dtype),
        in_specs=[pl.BlockSpec(memory_space=pltpu.SMEM), pl.BlockSpec(memory_space=pltpu.VMEM)],
        out_specs=pl.BlockSpec(memory_space=pltpu.VMEM),
        name="place",
    )(place, found)


def on_device(memory_rows, norm_gain, key_weight, owner_table):
    depth = lax.axis_size("grp") // 4
    row_count, width = memory_rows.shape
    order, place = tables(owner_table, depth)
    rows = memory_rows.reshape(row_count // BLK_ROWS, BLK_ROWS, width)
    found = refresh(depth, order, rows, norm_gain.reshape(1, -1), key_weight)
    out = place_blocks(place, found.reshape(row_count // BLK_ROWS, BLK_ROWS, width))
    return out.reshape(row_count, width)


def solution(mesh):
    in_specs = (P("grp", "tp"), P(), P(None, "tp"), P())
    out_specs = P("grp", "tp")
    return jax.shard_map(
        on_device, mesh=mesh, in_specs=in_specs, out_specs=out_specs, check_vma=False
    )
```

time: 237 us -> 93.1 us (0.39)
  waiting for transfers between devices: 157 us -> 0 us
  Pallas kernels: 0 us -> 89 us
  local copies, waits for them, and re-layouts: 34.9 us -> 0.01 us
  starting transfers between devices: 14.1 us -> 0 us
  between operations: 13.5 us -> 0.04 us
  matrix products: 7.74 us -> 0 us
  other arithmetic: 8.2 us -> 3.53 us
    all_gather x1 -> x0, waiting for transfers between devices: 134 us -> none  [project(): whole_rows = lax.all_gather(memory_rows, 'tp', axis=1, tiled=True)]
    pallas_call x0 -> x2, Pallas kernels: none -> 89 us  [the longest x1 86.6 us: refresh(): pl.pallas_call(functools.partial(refresh_kernel, depth), out_shape=jax.Sh...]
    scatter x1 -> x0, local copies, waits for them, and re-layouts: 30.5 us -> none  [to_owners(): inverse = jnp.zeros((block_total,), jnp.int32).at[owner_table].set(jnp.ar...]
    all_to_all x1 -> x0, waiting for transfers between devices: 22.3 us -> none  [to_owners(): lax.all_to_all(outgoing, 'grp', split_axis=0, concat_axis=0, tiled=True)]
    all_to_all x1 -> x0, starting transfers between devices: 14.1 us -> none  [to_owners(): lax.all_to_all(outgoing, 'grp', split_axis=0, concat_axis=0, tiled=True)]
    dot_general x3 -> x0, matrix products: 7.74 us -> none  [the longest x1 6.84 us: project(): keys = jnp.dot(normed, key_weight, preferred_element_type=jnp.float32)]
    reduce_sum x3 -> x4, other arithmetic: 6.43 us -> 2.52 us  [the longest x1 0.93 us: tables(): slot_first = jnp.sum(jnp.where(ids[None, :] == first, slot, 0), axis=1)]
  transfers between devices with their start and end apart: 2 -> 0, of which waited for: 2 -> 0; matrix products, arithmetic and copies ran while one was open for 14% -> 0% of each run, Pallas kernels for 0% -> 0%
where the time goes in v1:
time: 93.1 us; the launch traced here: 92.6 us
  Pallas kernels  89 us (96%)
  other arithmetic  3.53 us (4%)
    pallas_call x1, Pallas kernels, refresh(): pl.pallas_call(functools.partial(refresh_kernel, depth), out_shape=jax.Sh...  86.6 us
    pallas_call x1, Pallas kernels, place_blocks(): pl.pallas_call(place_kernel, out_shape=jax.ShapeDtypeStruct(found.shape,...  2.42 us

profile of v1, /device:TPU:1, one launch (start us, length us, event | category | flops | bytes accessed | tf_op | source)
XLA Modules:
  0.0 92.6 jit_solution(16454336128295208950)
XLA Ops:
  0.0 0.9 add_select_fusion.1
  1.0 0.2 convert_reduce_fusion
  1.1 0.7 select_reduce_fusion.order
  1.8 0.9 %select_reduce_fusion.3 = (s32[64]{0:T(128)S(1)}, s32[64]{0:T(128)S(1)}) fusion(s32[64]{0:T(128)S(1)} %get-tuple-element.8, s32[8192]{0:T(1024)} %param.7, s32[]{:T(128)S(6)} %axis_index.15), kind=kLoop, calls=%fused_computation.15 | loop fusion | flops 204672 | bytes 33540 | tf_op jit(solution)/shard_map/reduce_sum | solution.py:49
  2.8 0.1 pad_add_fusion
  2.9 0.7 select_reduce_fusion.1.place
  3.6 86.6 %refresh.1 = bf16[8,4,4,8,512]{4,3,2,1,0:T(8,128)(2,1)} custom-call(s32[128]{0:T(128)} %select_reduce_fusion.order, bf16[128,8,512]{2,1,0:T(8,128)(2,1)} %bitcast.43, f32[1,4096]{1,0:T(1,128)} %bitcast.44, bf16[4096,512]{1,0:T(8,128)(2,1)} %w_hbm.1), custom_call_target="tpu_custom_call" | custom-call | tf_op jit(solution)/shard_map/refresh/pallas_call | solution.py:362
  90.2 2.4 %place.1 = bf16[128,8,512]{2,1,0:T(8,128)(2,1)} custom-call(s32[128]{0:T(128)} %select_reduce_fusion.1.place, bf16[128,8,512]{2,1,0:T(8,128)(2,1)} %bitcast.42), custom_call_target="tpu_custom_call" | custom-call | tf_op jit(solution)/shard_map/place/pallas_call | solution.py:414
  (4 shorter events, 0.1 us)

commit v2 on v0

v2 whole, which is shorter than its diff:
```python
import functools

import jax
import jax.numpy as jnp
from jax import lax
from jax.experimental import pallas as pl
from jax.experimental.pallas import tpu as pltpu
from jax.sharding import PartitionSpec as P

BLK_ROWS = 8
EPS = 1e-05
MESH = pl.DeviceIdType.MESH

VMEM_LIMIT = 60 * 1024 * 1024
FIRST = 8
BURST = 2
W_PARTS = 4


def class_shift(q, depth):
    return lax.rem(((q + 1) // 2) * (2 * lax.rem(q, 2) - 1) + depth, depth)


def flip(bit, by):
    return 1 - bit if by else bit


def order_table(own, z, depth):
    blocks = own.shape[1]
    down = jnp.broadcast_to(own, (blocks, blocks)).T
    lane = lax.broadcasted_iota(jnp.int32, (blocks, blocks), 1)
    block = lax.broadcasted_iota(jnp.int32, (blocks, blocks), 0)
    q = lane >> 3
    shift = ((q + 1) >> 1) * (2 * (q & 1) - 1)
    dest = ((z + shift + depth) & (depth - 1)) * 4 + ((lane >> 1) & 3)
    hit = down == dest
    low = jnp.min(jnp.where(hit, block, blocks - 1), axis=0, keepdims=True)
    high = jnp.max(jnp.where(hit, block, 0), axis=0, keepdims=True)
    return jnp.where((lane[0:1] & 1) == 0, low, high)


def place_table(table, g, depth):
    groups, blocks = table.shape
    z, xl, co = g // 4, lax.rem(g // 2, 2), lax.rem(g, 2)
    bits = blocks.bit_length() - 1
    lane = lax.broadcasted_iota(jnp.int32, (groups, blocks), 1)
    src = lax.broadcasted_iota(jnp.int32, (groups, blocks), 0)
    mine = (table >> bits) == g
    slot = table & (blocks - 1)
    column = jnp.where(mine, lane, blocks).astype(jnp.float32)
    first = jnp.min(column, axis=1, keepdims=True).astype(jnp.int32)
    slot_f = slot.astype(jnp.float32)
    slot_first = jnp.sum(jnp.where(lane == first, slot_f, 0.0), axis=1, keepdims=True)
    slot_both = jnp.sum(jnp.where(mine, slot_f, 0.0), axis=1, keepdims=True)
    slot_first, slot_last = slot_first.astype(jnp.int32), (slot_both - slot_first).astype(jnp.int32)
    back = (z - (src >> 2) + depth) & (depth - 1)
    q = jnp.where(back <= depth // 2, jnp.maximum(2 * back - 1, 0), 2 * (depth - back))
    dl = (((src >> 1) & 1) + xl) & 1
    dc = ((src & 1) + co) & 1
    at = (((q >> 1) * 4 + dl * 2 + dc) * 2 + (q & 1)) * 2
    spot = jnp.where(slot_first == lane, at, jnp.where(slot_last == lane, at + 1, 0))
    found = jnp.sum(spot.astype(jnp.float32), axis=0, keepdims=True).astype(jnp.int32)
    return jnp.minimum(found, blocks - 1)


def refresh_kernel(
    depth,
    x_hbm,
    gain_hbm,
    w_hbm,
    table_hbm,
    found,
    place,
    xin,
    gain,
    table,
    order_v,
    order,
    sorted_rows,
    gat,
    w_own,
    w_far,
    stats,
    normed,
    part,
    arrived,
    load_sem,
    send_sem,
    w_recv,
    z_recv,
    y_recv,
    r_recv,
    s_recv,
    x_recv,
):
    g, t = lax.axis_index("grp"), lax.axis_index("tp")
    z, xl, co = g // 4, lax.rem(g // 2, 2), lax.rem(g, 2)
    xh, y = t // 4, lax.rem(t, 4)
    chunks, pairs = depth, depth // 2
    dl_width = x_hbm.shape[-1]
    features = 8 * dl_width
    half_rows = 4 * dl_width
    rows_c = 64

    def device(zz, xxl, cc, xxh, yy):
        return {"grp": zz * 4 + xxl * 2 + cc, "tp": xxh * 4 + yy}

    w_start = pl.multiple_of(xh * half_rows, half_rows)
    load_table = pltpu.make_async_copy(table_hbm, table, load_sem.at[0])
    load_table.start()
    load = pltpu.make_async_copy(x_hbm, xin, load_sem.at[1])
    load.start()

    barrier = pltpu.get_barrier_semaphore()
    partners = 0
    for step in range(1, depth):
        pl.semaphore_signal(
            barrier, inc=1, device_id=device(lax.rem(z + step, depth), xl, co, xh, y), device_id_type=MESH
        )
        partners += 1
    for step in range(1, 8):
        pl.semaphore_signal(
            barrier, inc=1, device_id={"grp": g, "tp": lax.rem(t + step, 8)}, device_id_type=MESH
        )
        partners += 1
    for j in range(1, 8):
        if j == 4:
            continue
        pl.semaphore_signal(
            barrier,
            inc=1,
            device_id=device(z, flip(xl, (j // 2) % 2), flip(co, j % 2), flip(xh, j // 4), y),
            device_id_type=MESH,
        )
        partners += 1

    load_table.wait()
    own = table[pl.ds(g, 1), :] >> ((8 * depth).bit_length() - 1)
    order_v[...] = order_table(own, z, depth)
    load_order = pltpu.make_async_copy(order_v, order, load_sem.at[2])
    load_order.start()
    load_gain = pltpu.make_async_copy(gain_hbm, gain, load_sem.at[3])
    load_gain.start()
    load_w = pltpu.make_async_copy(w_hbm.at[pl.ds(w_start, half_rows)], w_own, load_sem.at[4])
    load_w.start()
    load_order.wait()
    load.wait()

    def sort_class(q):
        for e in range(8):
            sorted_rows[q, e] = xin[order[0, q * 8 + e]]

    def z_copy(q):
        return pltpu.make_async_remote_copy(
            src_ref=sorted_rows.at[q],
            dst_ref=gat.at[y, q],
            send_sem=send_sem.at[0],
            recv_sem=z_recv.at[q],
            device_id=device(lax.rem(z + class_shift(q, depth), depth), xl, co, xh, y),
            device_id_type=MESH,
        )

    ahead = min(2, depth - 1)
    for q in range(1, 1 + ahead):
        sort_class(q)
    pl.semaphore_wait(barrier, partners)

    w_rows = half_rows // 4
    w_run = w_rows // W_PARTS

    def w_span(l, c, k):
        return pl.ds(pl.multiple_of((l * 2 + c) * w_rows + k * w_run, w_run), w_run)

    def w_first(k):
        start = (1 - xh) * half_rows + ((1 - xl) * 2 + co) * w_rows + k * w_run
        return pltpu.make_async_remote_copy(
            src_ref=w_hbm.at[pl.ds(pl.multiple_of(start, w_run), w_run)],
            dst_ref=w_far.at[w_span(1 - xl, co, k)],
            send_sem=send_sem.at[1],
            recv_sem=w_recv.at[0, k],
            device_id=device(z, 1 - xl, co, 1 - xh, y),
            device_id_type=MESH,
        )

    def w_pass(kind, k):
        span = w_span(1 - xl if kind == 3 else xl, co, k)
        to = device(z, 1 - xl, co, xh, y) if kind == 1 else device(z, xl, 1 - co, xh, y)
        return pltpu.make_async_remote_copy(
            src_ref=w_far.at[span],
            dst_ref=w_far.at[span],
            send_sem=send_sem.at[1],
            recv_sem=w_recv.at[kind, k],
            device_id=to,
            device_id_type=MESH,
        )

    for k in range(W_PARTS):
        w_first(k).start()

    def z_start(q, carry):
        z_copy(q).start()

        @pl.when(q + ahead < depth)
        def _():
            sort_class(q + ahead)

        return carry

    lax.fori_loop(1, depth, z_start, 0)
    for e in range(8):
        gat[y, 0, e] = xin[order[0, e]]
    place[...] = place_table(table[...], g, depth)

    left, right = lax.rem(y + 3, 4), lax.rem(y + 1, 4)

    def y_copy(side, c):
        return pltpu.make_async_remote_copy(
            src_ref=gat.at[y, c],
            dst_ref=gat.at[y, c],
            send_sem=send_sem.at[2],
            recv_sem=y_recv.at[c],
            device_id=device(z, xl, co, xh, right if side == 0 else left),
            device_id_type=MESH,
        )

    def relay_copy(side, c):
        span = pl.ds(0, 4) if side == 0 else pl.ds(4, 4)
        piece = left if side == 0 else right
        return pltpu.make_async_remote_copy(
            src_ref=gat.at[piece, c, span],
            dst_ref=gat.at[piece, c, span],
            send_sem=send_sem.at[3],
            recv_sem=r_recv.at[c],
            device_id=device(z, xl, co, xh, right if side == 0 else left),
            device_id_type=MESH,
        )

    def stats_copy(c, step):
        return pltpu.make_async_remote_copy(
            src_ref=stats.at[c, 0],
            dst_ref=stats.at[c, step],
            send_sem=send_sem.at[4],
            recv_sem=s_recv.at[c],
            device_id={"grp": g, "tp": lax.rem(t + step, 8)},
            device_id_type=MESH,
        )

    def x_copy(p, j):
        dh, dl, dc = j // 4, (j // 2) % 2, j % 2
        to_l, to_c = flip(xl, dl), flip(co, dc)
        return pltpu.make_async_remote_copy(
            src_ref=part.at[p, dh, :, to_l * 2 + to_c],
            dst_ref=arrived.at[p, j],
            send_sem=send_sem.at[5],
            recv_sem=x_recv.at[p],
            device_id=device(z, to_l, to_c, flip(xh, dh), y),
            device_id_type=MESH,
        )

    def take(c):
        @pl.when(c > 0)
        def _():
            z_copy(c).wait_recv()

        y_copy(0, c).start()
        y_copy(1, c).start()
        v = gat[y, c].astype(jnp.float32).reshape(rows_c, dl_width)
        row_sum = jnp.sum(v, axis=1, keepdims=True)
        row_sq = jnp.sum(v * v, axis=1, keepdims=True)
        lane = lax.broadcasted_iota(jnp.int32, (rows_c, 128), 1)
        both = jnp.where(lane == 0, row_sum, jnp.where(lane == 1, row_sq, 0.0))
        stats[c, 0, :, pl.ds(0, rows_c)] = both.T[0:8, :]
        for step in range(1, 8):
            stats_copy(c, step).start()

    def all_of(ref, sem):
        pltpu.make_async_copy(ref, ref, sem).wait()

    def relay(c):
        all_of(gat.at[pl.ds(0, 2), c], y_recv.at[c])
        relay_copy(0, c).start()
        relay_copy(1, c).start()

    def multiply(p):
        means, scales = [], []
        for k in range(2):
            c = 2 * p + k
            all_of(gat.at[0, c], r_recv.at[c])
            all_of(stats.at[c, pl.ds(1, 7)], s_recv.at[c])
            total = jnp.sum(stats[c], axis=0)[:, 0:rows_c]
            mean = total[0:1] / features
            var = total[1:2] / features - mean * mean
            rstd = lax.rsqrt(var + EPS)
            sub = lax.broadcasted_iota(jnp.int32, (128, rows_c), 0)
            columns = jnp.where(sub == 0, mean, rstd).T
            mean_c, rstd_c = columns[:, 0:1], columns[:, 1:2]
            for yy in range(4):
                v = gat[yy, c].astype(jnp.float32).reshape(rows_c, dl_width)
                scale = gain[0:1, pl.ds(pl.multiple_of(w_start + yy * dl_width, dl_width), dl_width)]
                normed[pl.ds(k * rows_c, rows_c), pl.ds(yy * dl_width, dl_width)] = (
                    (v - mean_c) * rstd_c * scale
                ).astype(jnp.bfloat16)
        shape = (2, 4, 2, BLK_ROWS, dl_width)
        for dh, weight in ((1, w_far), (0, w_own)):
            keys = jnp.dot(normed[...], weight[...], preferred_element_type=jnp.float32)
            part[p, dh] = keys.reshape(shape).astype(jnp.bfloat16)
            for j in range(max(1, 4 * dh), 4 * dh + 4):
                x_copy(p, j).start()

    def add(p):
        all_of(arrived.at[p, pl.ds(1, 7)], x_recv.at[p])
        for e in range(4):
            a = part[p, 0, :, xl * 2 + co] if e == 0 else arrived[p, e]
            b = arrived[p, 4 + e]
            found[p, e] = (a.astype(jnp.float32) + b.astype(jnp.float32)).astype(jnp.bfloat16)

    def done(i):
        ready = jnp.minimum(jnp.maximum((i - (FIRST - 1)) * BURST, 0), jnp.maximum(i - 2, 0) // 2)
        return jnp.minimum(ready, pairs)

    def loop(i, carry):
        @pl.when(jnp.logical_and(i >= 2, i <= chunks + 1))
        def _():
            relay(i - 2)

        @pl.when(jnp.logical_and(i >= 2, i < 2 + W_PARTS))
        def _():
            w_first(i - 2).wait_recv()
            w_pass(1, i - 2).start()
            w_pass(2, i - 2).start()

        @pl.when(jnp.logical_and(i >= 4, i < 4 + W_PARTS))
        def _():
            w_pass(1, i - 4).wait_recv()
            w_pass(3, i - 4).start()

        @pl.when(i == FIRST)
        def _():
            load_w.wait()
            load_gain.wait()
            for k in range(W_PARTS):
                w_pass(2, k).wait_recv()
                w_pass(3, k).wait_recv()

        @pl.when(i >= FIRST)
        def _():
            lax.fori_loop(done(i - 1), done(i), lambda p, a: (multiply(p), a)[1], 0)

        @pl.when(i >= FIRST + 1)
        def _():
            lax.fori_loop(done(i - 2), done(i - 1), lambda p, a: (add(p), a)[1], 0)

        @pl.when(i < chunks)
        def _():
            take(i)

        return carry

    lax.fori_loop(0, chunks + 4, loop, 0)

    all_of(sorted_rows.at[pl.ds(1, depth - 1)], send_sem.at[0])
    all_of(w_own, send_sem.at[1])
    all_of(gat.at[pl.ds(0, 2)], send_sem.at[2])
    all_of(gat.at[0], send_sem.at[3])
    all_of(stats.at[:, pl.ds(1, 7)], send_sem.at[4])
    all_of(arrived.at[:, pl.ds(1, 7)], send_sem.at[5])


def refresh(depth, rows, gain, weight, table):
    chunks, pairs = depth, depth // 2
    blocks, _, width = rows.shape
    bf16 = jnp.bfloat16
    dma = pltpu.SemaphoreType.DMA
    hbm_space = pl.BlockSpec(memory_space=pltpu.HBM)
    return pl.pallas_call(
        functools.partial(refresh_kernel, depth),
        out_shape=[
            jax.ShapeDtypeStruct((pairs, 4, 2, 2, BLK_ROWS, width), bf16),
            jax.ShapeDtypeStruct((1, blocks), jnp.int32),
        ],
        in_specs=[hbm_space] * 4,
        out_specs=[pl.BlockSpec(memory_space=pltpu.VMEM)] * 2,
        scratch_shapes=[
            pltpu.VMEM((blocks, BLK_ROWS, width), bf16),
            pltpu.VMEM(gain.shape, jnp.float32),
            pltpu.VMEM(table.shape, jnp.int32),
            pltpu.VMEM((1, blocks), jnp.int32),
            pltpu.SMEM((1, blocks), jnp.int32),
            pltpu.VMEM((chunks, 8, BLK_ROWS, width), bf16),
            pltpu.VMEM((4, chunks, 8, BLK_ROWS, width), bf16),
            pltpu.VMEM((4 * width, width), bf16),
            pltpu.VMEM((4 * width, width), bf16),
            pltpu.VMEM((chunks, 8, 8, 128), jnp.float32),
            pltpu.VMEM((128, 4 * width), bf16),
            pltpu.VMEM((pairs, 2, 2, 4, 2, BLK_ROWS, width), bf16),
            pltpu.VMEM((pairs, 8, 2, 2, BLK_ROWS, width), bf16),
            dma((5,)),
            dma((6,)),
            dma((4, W_PARTS)),
            dma((depth,)),
            dma((chunks,)),
            dma((chunks,)),
            dma((chunks,)),
            dma((pairs,)),
        ],
        compiler_params=pltpu.CompilerParams(
            collective_id=0, has_side_effects=True, vmem_limit_bytes=VMEM_LIMIT
        ),
        name="refresh",
    )(rows, gain, weight, table)


def place_kernel(place, found, out, placed, out_sem):
    blocks = placed.shape[0]
    run = blocks // 4

    def step(p, carry):
        placed[p] = found[place[0, p]]
        return carry

    def save(part):
        span = pl.ds(part * run, run)
        return pltpu.make_async_copy(placed.at[span], out.at[span], out_sem.at[part])

    for part in range(4):
        lax.fori_loop(part * run, (part + 1) * run, step, 0, unroll=8)
        save(part).start()
    for part in range(4):
        save(part).wait()


def place_blocks(place, found):
    return pl.pallas_call(
        place_kernel,
        out_shape=jax.ShapeDtypeStruct(found.shape, found.dtype),
        in_specs=[pl.BlockSpec(memory_space=pltpu.SMEM), pl.BlockSpec(memory_space=pltpu.VMEM)],
        out_specs=pl.BlockSpec(memory_space=pl.ANY),
        scratch_shapes=[pltpu.VMEM(found.shape, found.dtype), pltpu.SemaphoreType.DMA((4,))],
        compiler_params=pltpu.CompilerParams(vmem_limit_bytes=VMEM_LIMIT),
        name="place",
    )(place, found)


def on_device(memory_rows, norm_gain, key_weight, owner_table):
    groups = lax.axis_size("grp")
    row_count, width = memory_rows.shape
    blocks = row_count // BLK_ROWS
    rows = memory_rows.reshape(blocks, BLK_ROWS, width)
    table = owner_table.reshape(groups, blocks)
    found, place = refresh(groups // 4, rows, norm_gain.reshape(1, -1), key_weight, table)
    out = place_blocks(place, found.reshape(blocks, BLK_ROWS, width))
    return out.reshape(row_count, width)


def solution(mesh):
    in_specs = (P("grp", "tp"), P(), P(None, "tp"), P())
    out_specs = P("grp", "tp")
    return jax.shard_map(
        on_device, mesh=mesh, in_specs=in_specs, out_specs=out_specs, check_vma=False
    )
```

time: 237 us -> 88.4 us (0.37)
  waiting for transfers between devices: 157 us -> 0 us
  Pallas kernels: 0 us -> 87.6 us
  local copies, waits for them, and re-layouts: 34.9 us -> 0 us
  starting transfers between devices: 14.1 us -> 0 us
  between operations: 13.5 us -> 0.01 us
  other arithmetic: 8.2 us -> 0 us
  matrix products: 7.74 us -> 0 us
    all_gather x1 -> x0, waiting for transfers between devices: 134 us -> none  [project(): whole_rows = lax.all_gather(memory_rows, 'tp', axis=1, tiled=True)]
    pallas_call x0 -> x2, Pallas kernels: none -> 87.6 us  [the longest x1 85.3 us: refresh(): pl.pallas_call(functools.partial(refresh_kernel, depth), out_shape=[jax.S...]
    scatter x1 -> x0, local copies, waits for them, and re-layouts: 30.5 us -> none  [to_owners(): inverse = jnp.zeros((block_total,), jnp.int32).at[owner_table].set(jnp.ar...]
    all_to_all x1 -> x0, waiting for transfers between devices: 22.3 us -> none  [to_owners(): lax.all_to_all(outgoing, 'grp', split_axis=0, concat_axis=0, tiled=True)]
    all_to_all x1 -> x0, starting transfers between devices: 14.1 us -> none  [to_owners(): lax.all_to_all(outgoing, 'grp', split_axis=0, concat_axis=0, tiled=True)]
    dot_general x3 -> x0, matrix products: 7.74 us -> none  [the longest x1 6.84 us: project(): keys = jnp.dot(normed, key_weight, preferred_element_type=jnp.float32)]
    reduce_sum x3 -> x0, other arithmetic: 6.43 us -> none  [the longest x1 6.09 us: project(): row_mean = jnp.sum(values, axis=1, keepdims=True) / width]
  transfers between devices with their start and end apart: 2 -> 0, of which waited for: 2 -> 0; matrix products, arithmetic and copies ran while one was open for 14% -> 0% of each run, Pallas kernels for 0% -> 0%
where the time goes in v2:
time: 88.4 us; the launch traced here: 87.6 us
  Pallas kernels  87.6 us (99%)
    pallas_call x1, Pallas kernels, refresh(): pl.pallas_call(functools.partial(refresh_kernel, depth), out_shape=[jax.S...  85.3 us
    pallas_call x1, Pallas kernels, place_blocks(): pl.pallas_call(place_kernel, out_shape=jax.ShapeDtypeStruct(found.shape,...  2.28 us

profile of v2, /device:TPU:1, one launch (start us, length us, event | category | flops | bytes accessed | tf_op | source)
XLA Modules:
  0.0 87.6 jit_solution(14656501106546502926)
XLA Ops:
  0.0 85.3 %refresh.1 = (bf16[8,4,2,2,8,512]{5,4,3,2,1,0:T(8,128)(2,1)}, s32[1,128]{1,0:T(1,128)}) custom-call(bf16[128,8,512]{2,1,0:T(8,128)(2,1)} %bitcast.5, f32[1,4096]{1,0:T(1,128)} %bitcast.8, bf16[4096,512]{1,0:T(8,128)(2,1)} %w_hbm.1, s32[64,128]{1,0:T(8,128)} %bitcast.7), custom_call_target="tpu_custom_call" | custom-call | tf_op jit(solution)/shard_map/refresh/pallas_call | solution.py:375
  85.3 2.3 %place.1 = bf16[128,8,512]{2,1,0:T(8,128)(2,1)} custom-call(s32[1,128]{1,0:T(1,128)} %get-tuple-element.7.place, bf16[128,8,512]{2,1,0:T(8,128)(2,1)} %bitcast.6), custom_call_target="tpu_custom_call" | custom-call | tf_op jit(solution)/shard_map/place/pallas_call | solution.py:433

commit v3 on v2

--- a/solution.py
+++ b/solution.py
@@ -11,14 +11,25 @@
 EPS = 1e-05
 MESH = pl.DeviceIdType.MESH
 
-VMEM_LIMIT = 60 * 1024 * 1024
+VMEM_LIMIT = 40 * 1024 * 1024
 FIRST = 8
 BURST = 2
+LAG = 3
+EARLY = 4
 W_PARTS = 4
 
 
-def class_shift(q, depth):
-    return lax.rem(((q + 1) // 2) * (2 * lax.rem(q, 2) - 1) + depth, depth)
+def shifts(depth):
+    near = [n for step in range(1, depth // 2) for n in (step, -step)]
+    far = [0, depth // 2] + near[::-1][: EARLY - 2]
+    return far + near[: len(near) - (EARLY - 2)]
+
+
+def look_up(index, values):
+    out = jnp.zeros_like(index)
+    for at, value in enumerate(values):
+        out = jnp.where(index == at, value, out)
+    return out
 
 
 def flip(bit, by):
@@ -31,8 +42,7 @@
     lane = lax.broadcasted_iota(jnp.int32, (blocks, blocks), 1)
     block = lax.broadcasted_iota(jnp.int32, (blocks, blocks), 0)
     q = lane >> 3
-    shift = ((q + 1) >> 1) * (2 * (q & 1) - 1)
-    dest = ((z + shift + depth) & (depth - 1)) * 4 + ((lane >> 1) & 3)
+    dest = ((z + look_up(q, shifts(depth)) + depth) & (depth - 1)) * 4 + ((lane >> 1) & 3)
     hit = down == dest
     low = jnp.min(jnp.where(hit, block, blocks - 1), axis=0, keepdims=True)
     high = jnp.max(jnp.where(hit, block, 0), axis=0, keepdims=True)
@@ -54,7 +64,8 @@
     slot_both = jnp.sum(jnp.where(mine, slot_f, 0.0), axis=1, keepdims=True)
     slot_first, slot_last = slot_first.astype(jnp.int32), (slot_both - slot_first).astype(jnp.int32)
     back = (z - (src >> 2) + depth) & (depth - 1)
-    q = jnp.where(back <= depth // 2, jnp.maximum(2 * back - 1, 0), 2 * (depth - back))
+    chunk_of = {n % depth: q for q, n in enumerate(shifts(depth))}
+    q = look_up(back, [chunk_of[n] for n in range(depth)])
     dl = (((src >> 1) & 1) + xl) & 1
     dc = ((src & 1) + co) & 1
     at = (((q >> 1) * 4 + dl * 2 + dc) * 2 + (q & 1)) * 2
@@ -84,6 +95,8 @@
     normed,
     part,
     arrived,
+    leaving,
+    landed,
     load_sem,
     send_sem,
     w_recv,
@@ -156,12 +169,11 @@
             dst_ref=gat.at[y, q],
             send_sem=send_sem.at[0],
             recv_sem=z_recv.at[q],
-            device_id=device(lax.rem(z + class_shift(q, depth), depth), xl, co, xh, y),
-            device_id_type=MESH,
-        )
-
-    ahead = min(2, depth - 1)
-    for q in range(1, 1 + ahead):
+            device_id=device(lax.rem(z + shifts(depth)[q] + depth, depth), xl, co, xh, y),
+            device_id_type=MESH,
+        )
+
+    for q in range(EARLY, EARLY + 2):
         sort_class(q)
     pl.semaphore_wait(barrier, partners)
 
@@ -197,18 +209,13 @@
     for k in range(W_PARTS):
         w_first(k).start()
 
-    def z_start(q, carry):
+    for q in range(EARLY, depth):
         z_copy(q).start()
-
-        @pl.when(q + ahead < depth)
-        def _():
-            sort_class(q + ahead)
-
-        return carry
-
-    lax.fori_loop(1, depth, z_start, 0)
-    for e in range(8):
-        gat[y, 0, e] = xin[order[0, e]]
+        if q + 2 < depth:
+            sort_class(q + 2)
+    for q in range(EARLY):
+        for e in range(8):
+            gat[y, q, e] = xin[order[0, q * 8 + e]]
     place[...] = place_table(table[...], g, depth)
 
     left, right = lax.rem(y + 3, 4), lax.rem(y + 1, 4)
@@ -257,10 +264,23 @@
             device_id_type=MESH,
         )
 
+    def all_of(ref, sem):
+        pltpu.make_async_copy(ref, ref, sem).wait()
+
+    def key_copy(q):
+        return pltpu.make_async_remote_copy(
+            src_ref=leaving.at[q // 2, :, q % 2],
+            dst_ref=landed.at[q // 2, :, q % 2],
+            send_sem=send_sem.at[0],
+            recv_sem=z_recv.at[q],
+            device_id=device(lax.rem(z + shifts(depth)[q] + depth, depth), xl, co, xh, y),
+            device_id_type=MESH,
+        )
+
     def take(c):
-        @pl.when(c > 0)
-        def _():
-            z_copy(c).wait_recv()
+        @pl.when(c >= EARLY)
+        def _():
+            all_of(gat.at[0, c], z_recv.at[c])
 
         y_copy(0, c).start()
         y_copy(1, c).start()
@@ -269,12 +289,11 @@
         row_sq = jnp.sum(v * v, axis=1, keepdims=True)
         lane = lax.broadcasted_iota(jnp.int32, (rows_c, 128), 1)
         both = jnp.where(lane == 0, row_sum, jnp.where(lane == 1, row_sq, 0.0))
-        stats[c, 0, :, pl.ds(0, rows_c)] = both.T[0:8, :]
+        flat = both.T
+        stats[c, 0, :, pl.ds(0, rows_c)] = flat[0:1, :]
+        stats[c, 0, :, pl.ds(rows_c, rows_c)] = flat[1:2, :]
         for step in range(1, 8):
             stats_copy(c, step).start()
-
-    def all_of(ref, sem):
-        pltpu.make_async_copy(ref, ref, sem).wait()
 
     def relay(c):
         all_of(gat.at[pl.ds(0, 2), c], y_recv.at[c])
@@ -287,9 +306,9 @@
             c = 2 * p + k
             all_of(gat.at[0, c], r_recv.at[c])
             all_of(stats.at[c, pl.ds(1, 7)], s_recv.at[c])
-            total = jnp.sum(stats[c], axis=0)[:, 0:rows_c]
-            mean = total[0:1] / features
-            var = total[1:2] / features - mean * mean
+            total = jnp.sum(stats[c], axis=0)
+            mean = total[:, 0:rows_c] / features
+            var = total[:, rows_c : 2 * rows_c] / features - mean * mean
             rstd = lax.rsqrt(var + EPS)
             sub = lax.broadcasted_iota(jnp.int32, (128, rows_c), 0)
             columns = jnp.where(sub == 0, mean, rstd).T
@@ -312,17 +331,25 @@
         for e in range(4):
             a = part[p, 0, :, xl * 2 + co] if e == 0 else arrived[p, e]
             b = arrived[p, 4 + e]
-            found[p, e] = (a.astype(jnp.float32) + b.astype(jnp.float32)).astype(jnp.bfloat16)
+            keys = (a.astype(jnp.float32) + b.astype(jnp.float32)).astype(jnp.bfloat16)
+            found[p, e] = keys
+
+            @pl.when(p < EARLY // 2)
+            def _():
+                leaving[p, e] = keys
+
+        for early in range(EARLY // 2):
+
+            @pl.when(p == early)
+            def _():
+                for q in range(max(1, 2 * early), 2 * early + 2):
+                    key_copy(q).start()
 
     def done(i):
         ready = jnp.minimum(jnp.maximum((i - (FIRST - 1)) * BURST, 0), jnp.maximum(i - 2, 0) // 2)
         return jnp.minimum(ready, pairs)
 
     def loop(i, carry):
-        @pl.when(jnp.logical_and(i >= 2, i <= chunks + 1))
-        def _():
-            relay(i - 2)
-
         @pl.when(jnp.logical_and(i >= 2, i < 2 + W_PARTS))
         def _():
             w_first(i - 2).wait_recv()
@@ -346,9 +373,13 @@
         def _():
             lax.fori_loop(done(i - 1), done(i), lambda p, a: (multiply(p), a)[1], 0)
 
-        @pl.when(i >= FIRST + 1)
-        def _():
-            lax.fori_loop(done(i - 2), done(i - 1), lambda p, a: (add(p), a)[1], 0)
+        @pl.when(jnp.logical_and(i >= 2, i <= chunks + 1))
+        def _():
+            relay(i - 2)
+
+        @pl.when(i >= FIRST + LAG)
+        def _():
+            lax.fori_loop(done(i - LAG - 1), done(i - LAG), lambda p, a: (add(p), a)[1], 0)
 
         @pl.when(i < chunks)
         def _():
@@ -356,7 +387,11 @@
 
         return carry
 
-    lax.fori_loop(0, chunks + 4, loop, 0)
+    lax.fori_loop(0, chunks + 3 + LAG, loop, 0)
+
+    for q in range(1, EARLY):
+        all_of(gat.at[0, q], z_recv.at[q])
+        found[q // 2, :, q % 2] = landed[q // 2, :, q % 2]
 
     all_of(sorted_rows.at[pl.ds(1, depth - 1)], send_sem.at[0])
     all_of(w_own, send_sem.at[1])
@@ -390,10 +425,12 @@
             pltpu.VMEM((4, chunks, 8, BLK_ROWS, width), bf16),
             pltpu.VMEM((4 * width, width), bf16),
             pltpu.VMEM((4 * width, width), bf16),
-            pltpu.VMEM((chunks, 8, 8, 128), jnp.float32),
+            pltpu.VMEM((chunks, 8, 1, 128), jnp.float32),
             pltpu.VMEM((128, 4 * width), bf16),
             pltpu.VMEM((pairs, 2, 2, 4, 2, BLK_ROWS, width), bf16),
             pltpu.VMEM((pairs, 8, 2, 2, BLK_ROWS, width), bf16),
+            pltpu.VMEM((EARLY // 2, 4, 2, 2, BLK_ROWS, width), bf16),
+            pltpu.VMEM((EARLY // 2, 4, 2, 2, BLK_ROWS, width), bf16),
             dma((5,)),
             dma((6,)),
             dma((4, W_PARTS)),
@@ -407,7 +444,7 @@
             collective_id=0, has_side_effects=True, vmem_limit_bytes=VMEM_LIMIT
         ),
         name="refresh",
-    )(rows, gain, weight, table)
+    )(*(pltpu.with_memory_space_constraint(a, pltpu.HBM) for a in (rows, gain, weight, table)))
 
 
 def place_kernel(place, found, out, placed, out_sem):
@@ -436,7 +473,7 @@
         in_specs=[pl.BlockSpec(memory_space=pltpu.SMEM), pl.BlockSpec(memory_space=pltpu.VMEM)],
         out_specs=pl.BlockSpec(memory_space=pl.ANY),
         scratch_shapes=[pltpu.VMEM(found.shape, found.dtype), pltpu.SemaphoreType.DMA((4,))],
-        compiler_params=pltpu.CompilerParams(vmem_limit_bytes=VMEM_LIMIT),
+        compiler_params=pltpu.CompilerParams(vmem_limit_bytes=4 * 1024 * 1024),
         name="place",
     )(place, found)
 

time: 88.4 us -> 79.2 us (0.90)
  Pallas kernels: 87.6 us -> 79 us
    pallas_call x1, Pallas kernels: 85.3 us -> 77.5 us  [refresh(): pl.pallas_call(functools.partial(refresh_kernel, depth), out_shape=[jax.S...]
where the time goes in v3:
time: 79.2 us; the launch traced here: 79.1 us
  Pallas kernels  79 us (100%)
    pallas_call x1, Pallas kernels, refresh(): pl.pallas_call(functools.partial(refresh_kernel, depth), out_shape=[jax.S...  77.5 us
    pallas_call x1, Pallas kernels, place_blocks(): pl.pallas_call(place_kernel, out_shape=jax.ShapeDtypeStruct(found.shape,...  1.59 us

profile of v3, /device:TPU:1, one launch (start us, length us, event | category | flops | bytes accessed | tf_op | source)
XLA Modules:
  0.0 79.1 jit_solution(3503730303592595534)
XLA Ops:
  0.0 77.5 %refresh.1 = (bf16[8,4,2,2,8,512]{5,4,3,2,1,0:T(8,128)(2,1)S(1)}, s32[1,128]{1,0:T(1,128)S(1)}) custom-call(bf16[128,8,512]{2,1,0:T(8,128)(2,1)} %bitcast.6, f32[1,4096]{1,0:T(1,128)} %bitcast.8, bf16[4096,512]{1,0:T(8,128)(2,1)} %w_hbm.1, s32[64,128]{1,0:T(8,128)} %bitcast.7), custom_call_target="tpu_custom_call" | custom-call | tf_op jit(solution)/shard_map/refresh/pallas_call | solution.py:410
  77.5 1.6 %place.1 = bf16[128,8,512]{2,1,0:T(8,128)(2,1)} custom-call(s32[1,128]{1,0:T(1,128)S(1)} %get-tuple-element.7.place, bf16[128,8,512]{2,1,0:T(8,128)(2,1)S(1)} %bitcast.5), custom_call_target="tpu_custom_call" | custom-call | tf_op jit(solution)/shard_map/place/pallas_call | solution.py:470

commit v4 on v3

--- a/solution.py
+++ b/solution.py
@@ -13,9 +13,14 @@
 
 VMEM_LIMIT = 40 * 1024 * 1024
 FIRST = 8
-BURST = 2
+BURST = 3
 LAG = 3
 EARLY = 4
+LEAD = 3
+RELAY = 0
+MATMUL = 3
+W_ONE = 2
+W_TWO = 4
 W_PARTS = 4
 
 
@@ -346,20 +351,20 @@
                     key_copy(q).start()
 
     def done(i):
-        ready = jnp.minimum(jnp.maximum((i - (FIRST - 1)) * BURST, 0), jnp.maximum(i - 2, 0) // 2)
+        ready = jnp.minimum(jnp.maximum((i - (FIRST - 1)) * BURST, 0), jnp.maximum(i - (MATMUL - 1), 0) // 2)
         return jnp.minimum(ready, pairs)
 
     def loop(i, carry):
-        @pl.when(jnp.logical_and(i >= 2, i < 2 + W_PARTS))
-        def _():
-            w_first(i - 2).wait_recv()
-            w_pass(1, i - 2).start()
-            w_pass(2, i - 2).start()
-
-        @pl.when(jnp.logical_and(i >= 4, i < 4 + W_PARTS))
-        def _():
-            w_pass(1, i - 4).wait_recv()
-            w_pass(3, i - 4).start()
+        @pl.when(jnp.logical_and(i >= W_ONE, i < W_ONE + W_PARTS))
+        def _():
+            w_first(i - W_ONE).wait_recv()
+            w_pass(1, i - W_ONE).start()
+            w_pass(2, i - W_ONE).start()
+
+        @pl.when(jnp.logical_and(i >= W_TWO, i < W_TWO + W_PARTS))
+        def _():
+            w_pass(1, i - W_TWO).wait_recv()
+            w_pass(3, i - W_TWO).start()
 
         @pl.when(i == FIRST)
         def _():
@@ -373,21 +378,22 @@
         def _():
             lax.fori_loop(done(i - 1), done(i), lambda p, a: (multiply(p), a)[1], 0)
 
-        @pl.when(jnp.logical_and(i >= 2, i <= chunks + 1))
-        def _():
-            relay(i - 2)
+        @pl.when(jnp.logical_and(i >= RELAY, i < chunks + RELAY))
+        def _():
+            relay(i - RELAY)
 
         @pl.when(i >= FIRST + LAG)
         def _():
             lax.fori_loop(done(i - LAG - 1), done(i - LAG), lambda p, a: (add(p), a)[1], 0)
 
-        @pl.when(i < chunks)
-        def _():
-            take(i)
+        @pl.when(i < chunks - LEAD)
+        def _():
+            take(i + LEAD)
 
         return carry
 
-    lax.fori_loop(0, chunks + 3 + LAG, loop, 0)
+    lax.fori_loop(0, LEAD, lambda c, a: (take(c), a)[1], 0)
+    lax.fori_loop(0, chunks + MATMUL + LAG, loop, 0)
 
     for q in range(1, EARLY):
         all_of(gat.at[0, q], z_recv.at[q])

time: 79.2 us -> 69.1 us (0.87)
  Pallas kernels: 79 us -> 69 us
    pallas_call x1, Pallas kernels: 77.5 us -> 67.4 us  [refresh(): pl.pallas_call(functools.partial(refresh_kernel, depth), out_shape=[jax.S...]
where the time goes in v4:
time: 69.1 us; the launch traced here: 69 us
  Pallas kernels  69 us (100%)
    pallas_call x1, Pallas kernels, refresh(): pl.pallas_call(functools.partial(refresh_kernel, depth), out_shape=[jax.S...  67.4 us
    pallas_call x1, Pallas kernels, place_blocks(): pl.pallas_call(place_kernel, out_shape=jax.ShapeDtypeStruct(found.shape,...  1.59 us

profile of v4, /device:TPU:1, one launch (start us, length us, event | category | flops | bytes accessed | tf_op | source)
XLA Modules:
  0.0 69.0 jit_solution(4695078651126790872)
XLA Ops:
  0.0 67.4 %refresh.1 = (bf16[8,4,2,2,8,512]{5,4,3,2,1,0:T(8,128)(2,1)S(1)}, s32[1,128]{1,0:T(1,128)S(1)}) custom-call(bf16[128,8,512]{2,1,0:T(8,128)(2,1)} %bitcast.6, f32[1,4096]{1,0:T(1,128)} %bitcast.8, bf16[4096,512]{1,0:T(8,128)(2,1)} %w_hbm.1, s32[64,128]{1,0:T(8,128)} %bitcast.7), custom_call_target="tpu_custom_call" | custom-call | tf_op jit(solution)/shard_map/refresh/pallas_call | solution.py:416
  67.4 1.6 %place.1 = bf16[128,8,512]{2,1,0:T(8,128)(2,1)} custom-call(s32[1,128]{1,0:T(1,128)S(1)} %get-tuple-element.7.place, bf16[128,8,512]{2,1,0:T(8,128)(2,1)S(1)} %bitcast.5), custom_call_target="tpu_custom_call" | custom-call | tf_op jit(solution)/shard_map/place/pallas_call | solution.py:476
